TPU v7x, 32 devices: a whole 2x2x4 slice. The times are simulated.
32 devices in a mesh: rows: 32 (over z, y, x, core).
Axes of the slice: x: 2, y: 2, z: 4, core: 2. Of those that a mesh axis runs over, the one named last changes fastest.
Arguments:
- edge_tiles: bfloat16 [8192, 128, 128], P('rows'), may hold values from -0.5 to 0.5
- tile_row: int32 [8192], P('rows'), may hold values from 0 to 7
- tile_slot: int32 [8192], P('rows'), may hold values from 0 to 63, as said below
- tile_count: int32 [32], P('rows'), may hold values from 32 to 256, as said below
- fetch_list: int32 [32, 64], P('rows'), may hold values from 0 to 7, as said below
- hub_start: float32 [8, 32768], P(None, 'rows'), may hold values from -6 to 6
Outputs:
- hub: float32 [8, 32768], P(None, 'rows')
- authority: float32 [8, 32768], P(None, 'rows')
Inputs may be any that keep to these rules, and one draw needn't show every extreme that they name: tile_slot[t] = p * 2 + k names entry k of the fetch_list group of device p, in the row of the tile's own device. `fetch_list`: entries p * 2 to p * 2 + 1 of each row are 2 distinct block numbers among device p's own 8 blocks. Tile slots of device d at positions 256 * d + i with i >= tile_count[d] are not part of the graph.
All inputs are finite; a program needn't handle non-finite values.
Results may differ from a plain program's by a relative error of at most 0.004.
Values may be sent and summed in bfloat16 or wider, within the bound.
No kernel may reach another device: no remote copies, remote signals or barrier semaphores. Data moves between devices by JAX's collectives and lax.ppermute only.
A program may use at most 64 MiB of HBM per device.

v0:
```python
import jax
import jax.numpy as jnp
from jax import lax
from jax.sharding import PartitionSpec as P

ITERS = 2


def square_sums(raw_blocks):
    return jnp.sum(raw_blocks * raw_blocks, axis=(0, 2))


def rescale(raw_blocks, sums, node_total):
    return raw_blocks / jnp.sqrt(sums / node_total + 1e-06)[None, :, None]


def hub_norm_sum(hub_raw):
    return lax.psum(square_sums(hub_raw), "rows")


def per_device(edge_tiles, tile_row, tile_slot, tile_count, fetch_list, hub_start):
    devices = lax.axis_size("rows")
    tile_total = edge_tiles.shape[0]
    tile_edge = edge_tiles.shape[1]
    columns = hub_start.shape[0]
    block_local = hub_start.shape[1] // tile_edge
    slot_total = fetch_list.shape[1]
    slots_each = slot_total // devices
    node_total = hub_start.shape[1] * devices
    group_size = min(64, tile_total)
    live_count = tile_count[0]
    rounds = (live_count + group_size - 1) // group_size
    wanted_local = fetch_list[0]
    block_ids = jnp.arange(block_local, dtype=jnp.int32)

    def group_inputs(group_index):
        first_tile = group_index * group_size
        tiles_now = lax.dynamic_slice_in_dim(edge_tiles, first_tile, group_size, 0)
        rows_now = lax.dynamic_slice_in_dim(tile_row, first_tile, group_size, 0)
        slots_now = lax.dynamic_slice_in_dim(tile_slot, first_tile, group_size, 0)
        alive_mask = (first_tile + jnp.arange(group_size, dtype=jnp.int32) < live_count).astype(
            jnp.float32
        )
        return (tiles_now, rows_now, slots_now, alive_mask)

    owner_wanted = lax.all_to_all(
        wanted_local.reshape(devices, slots_each), "rows", split_axis=0, concat_axis=0, tiled=True
    ).reshape(slot_total)
    owner_selector = (block_ids[:, None] == owner_wanted[None, :]).astype(jnp.float32)
    hub_blocks = hub_start.reshape(columns, block_local, tile_edge).transpose(1, 0, 2)
    hub_low = hub_blocks.astype(jnp.bfloat16)
    authority_blocks = hub_blocks
    for sweep in range(ITERS):

        def transpose_accumulate(group_index, partial_value):
            tiles_now, rows_now, slots_now, alive_mask = group_inputs(group_index)
            source = jnp.take(hub_low, rows_now, axis=0)
            product = jnp.einsum(
                "gce,gef->gcf", source, tiles_now, preferred_element_type=jnp.float32
            )
            product = product * alive_mask[:, None, None]
            return partial_value + jax.ops.segment_sum(product, slots_now, num_segments=slot_total)

        transpose_start_value = jnp.zeros((slot_total, columns, tile_edge), jnp.float32)
        partial_value = lax.fori_loop(0, rounds, transpose_accumulate, transpose_start_value)
        returned = lax.all_to_all(
            partial_value.reshape(devices, slots_each, columns, tile_edge),
            "rows",
            split_axis=0,
            concat_axis=0,
            tiled=True,
        )
        returned = returned.reshape(slot_total, columns, tile_edge)
        authority_raw = jnp.einsum(
            "bs,scx->bcx", owner_selector, returned, precision=lax.Precision.HIGHEST
        )
        authority_low = authority_raw.astype(jnp.bfloat16)
        reply = jnp.take(authority_low, owner_wanted, axis=0).reshape(
            devices, slots_each, columns, tile_edge
        )
        fetched = lax.all_to_all(reply, "rows", split_axis=0, concat_axis=0, tiled=True).reshape(
            slot_total, columns, tile_edge
        )
        final_sweep = sweep + 1 == ITERS
        if final_sweep:
            authority_sums = lax.psum(square_sums(authority_raw), "rows")

        def forward_accumulate(group_index, partial_value):
            tiles_now, rows_now, slots_now, alive_mask = group_inputs(group_index)
            source = jnp.take(fetched, slots_now, axis=0)
            product = jnp.einsum(
                "gcf,gef->gce", source, tiles_now, preferred_element_type=jnp.float32
            )
            selector = (block_ids[:, None] == rows_now[None, :]).astype(jnp.float32) * alive_mask[
                None, :
            ]
            return partial_value + jnp.einsum(
                "bg,gcx->bcx", selector, product, precision=lax.Precision.HIGHEST
            )

        start_value = jnp.zeros((block_local, columns, tile_edge), jnp.float32)
        hub_raw = lax.fori_loop(0, rounds, forward_accumulate, start_value)
        if final_sweep:
            hub_sums = hub_norm_sum(hub_raw)
            authority_blocks = rescale(authority_raw, authority_sums, node_total)
        else:
            hub_sums = hub_norm_sum(hub_raw)
        hub_blocks = rescale(hub_raw, hub_sums, node_total)
        hub_low = hub_blocks.astype(jnp.bfloat16)
    hub = hub_blocks.transpose(1, 0, 2).reshape(columns, block_local * tile_edge)
    authority = authority_blocks.transpose(1, 0, 2).reshape(columns, block_local * tile_edge)
    return (hub, authority)


def solution(mesh):
    in_specs = (
        P("rows", None, None),
        P("rows"),
        P("rows"),
        P("rows"),
        P("rows", None),
        P(None, "rows"),
    )
    out_specs = (P(None, "rows"), P(None, "rows"))
    return jax.shard_map(
        per_device, mesh=mesh, in_specs=in_specs, out_specs=out_specs, check_vma=False
    )
```

profile of v0, /device:TPU:0, one launch (start us, length us, event | category | flops | bytes accessed | tf_op | source)
XLA Modules:
  0.0 253.3 jit_solution(3191059384154853317)
XLA Ops:
  3.2 7.3 %all-to-all-start = ((s32[32,1,2]{2,1,0:T(1,128)}), s32[32,1,2]{2,1,0:T(1,128)S(1)}, u32[]{:S(2)}, u32[]{:S(2)}) async-start(s32[32,1,2]{2,1,0:T(1,128)} %bitcast.1), calls=%async_computation | async-start | bytes 32768 | tf_op jit(solution)/shard_map/all_to_all | solution.py:46
  12.0 7.9 %while.42 = (s32[]{:T(128)}, f32[64,8,128]{2,1,0:T(8,128)S(1)}, s32[]{:T(128)}, s32[256]{0:T(256)}, s32[256]{0:T(256)}, /*index=5*/bf16[8,8,128]{2,1,0:T(8,128)(...) while((s32[]{:T(128)}, f32[64,8,128]{2,1,0:T(8,128)S(1)}, ...), condition=%wide.region_2.4_spmd, body=%wide.region_0.3_spmd.sunk | while | flops 16975428 | bytes 3545655 | solution.py:65
  12.0 1.4 compare_and_fusion.9
  14.1 2.3 fusion.78
  17.1 2.7 %scatter_fusion = f32[64,8,128]{2,1,0:T(8,128)S(1)} fusion(f32[64,8,128]{2,1,0:T(8,128)S(1)} %get-tuple-element.581, s32[64]{0:T(128)S(1)} %dynamic_slice.71, f32[64,8,128]{2,1,0:T(8,128)S(1)} %fusion.78), kind=kCustom, calls=%fused_computation.6.clone.1 | custom fusion | flops 65536 | bytes 786688 | tf_op jit(solution)/shard_map/while/body/scatter-add | solution.py:62
  20.7 29.5 %all-to-all-start.1 = ((f32[32,2,8,128]{3,1,2,0:T(2,128)}), f32[32,2,8,128]{3,1,2,0:T(2,128)S(1)}, u32[]{:S(2)}, u32[]{:S(2)}) async-start(f32[32,2,8,128]{3,1,2,0:T(2,128)} %copy.29), calls=%async_computation.1 | async-start | bytes 524288 | tf_op jit(solution)/shard_map/all_to_all | solution.py:66
  51.0 9.8 %all-to-all-done.1 = f32[32,2,8,128]{3,1,2,0:T(2,128)S(1)} async-done(((f32[32,2,8,128]{3,1,2,0:T(2,128)}), f32[32,2,8,128]{3,1,2,0:T(2,128)S(1)}, u32[]{:S(2)}, u32[]{:S(2)}) %all-to-all-start.1) | async-done | bytes 262176 | tf_op jit(solution)/shard_map/all_to_all | solution.py:66
  62.5 2.6 %all-to-all-start.2 = ((bf16[32,2,8,128]{3,2,1,0:T(8,128)(2,1)}), bf16[32,2,8,128]{3,2,1,0:T(8,128)(2,1)S(1)}, u32[]{:S(2)}, u32[]{:S(2)}) async-start(bf16[32,2,8,128]{3,2,1,0:T(8,128)(2,1)} %bitcast.7), calls=%async_computation.2 | async-start | bytes 262144 | tf_op jit(solution)/shard_map/all_to_all | solution.py:81
  65.1 8.2 %all-to-all-done.2 = bf16[32,2,8,128]{3,2,1,0:T(8,128)(2,1)S(1)} async-done(((bf16[32,2,8,128]{3,2,1,0:T(8,128)(2,1)}), bf16[32,2,8,128]{3,2,1,0:T(8,128)(2,1)S(1)}, u32[]{:S(2)}, u32[]{:S(2)}) %all-to-all-start.2) | async-done | bytes 131104 | tf_op jit(solution)/shard_map/all_to_all | solution.py:81
  73.3 5.9 %while.44 = (s32[]{:T(128)}, f32[8,8,128]{2,0,1:T(8,128)S(1)}, s32[]{:T(128)}, s32[256]{0:T(256)}, s32[]{:T(128)}, /*index=5*/s32[256]{0:T(256)}, bf16[64,8,128]...) while((s32[]{:T(128)}, f32[8,8,128]{2,0,1:T(8,128)S(1)}, ...), condition=%wide.region_4.8_spmd.clone, body=%wide.region_3.7_spmd.clone.sunk | while | flops 23145028 | bytes 3086903 | solution.py:102
  73.3 1.4 compare_and_fusion.11
  75.3 2.8 %fusion.86 = f32[64,8,128]{2,1,0:T(8,128)S(1)} fusion(bf16[256,128,128]{2,1,0:T(8,128)(2,1)} %get-tuple-element.635, s32[]{:T(128)S(6)} %select_n.100, bf16[64,8,128]{2,1,0:T(8,128)(2,1)S(1)} %gather_fusion.2, pred[64]{0:T(512)(128)(4,1)S(1)} %get-tuple-element.555), kind=kOutput, calls=%fused_computation.34.clone.1 | convolution fusion | flops 16842752 | bytes 2490436 | tf_op jit(solution)/shard_map/while/body/gcf,gef->gce/dot_general | solution.py:91
  79.3 53.6 %psum.21 = f32[8]{0:T(128)S(1)} all-reduce(f32[8]{0:T(128)S(1)} %multiply_reduce_fusion.2), channel_id=1, replica_groups=mesh['rows'=32] {'rows'}, use_global_device_ids=true, to_apply=%region_6.10 | all-reduce | flops 8 | bytes 64 | tf_op jit(solution)/shard_map/psum | solution.py:18
  133.1 7.9 %while.43 = (s32[]{:T(128)}, f32[64,8,128]{2,1,0:T(8,128)S(1)}, s32[]{:T(128)}, s32[256]{0:T(256)}, s32[256]{0:T(256)}, /*index=5*/bf16[8,8,128]{2,1,0:T(8,128)(...) while((s32[]{:T(128)}, f32[64,8,128]{2,1,0:T(8,128)S(1)}, ...), condition=%wide.region_9.13_spmd, body=%wide.region_7.12_spmd.sunk | while | flops 16975428 | bytes 3545655 | solution.py:65
  133.1 1.4 compare_and_fusion.10
  135.2 2.3 fusion.81
  138.2 2.7 %scatter_fusion.1 = f32[64,8,128]{2,1,0:T(8,128)S(1)} fusion(f32[64,8,128]{2,1,0:T(8,128)S(1)} %get-tuple-element.653, s32[64]{0:T(128)S(1)} %dynamic_slice.73, f32[64,8,128]{2,1,0:T(8,128)S(1)} %fusion.81), kind=kCustom, calls=%fused_computation.7.clone.1 | custom fusion | flops 65536 | bytes 786688 | tf_op jit(solution)/shard_map/while/body/scatter-add | solution.py:62
  141.2 38.4 %all_to_all.29 = f32[32,2,8,128]{3,1,2,0:T(2,128)S(1)} all-to-all(f32[32,2,8,128]{3,1,2,0:T(2,128)S(1)} %copy.33), channel_id=1, replica_groups=mesh['rows'=32] {'rows'}, dimensions={0} | all-to-all | bytes 524288 | tf_op jit(solution)/shard_map/all_to_all | solution.py:66
  181.4 2.6 %all-to-all-start.4 = ((bf16[32,2,8,128]{3,2,1,0:T(8,128)(2,1)}), bf16[32,2,8,128]{3,2,1,0:T(8,128)(2,1)S(1)}, u32[]{:S(2)}, u32[]{:S(2)}) async-start(bf16[32,2,8,128]{3,2,1,0:T(8,128)(2,1)} %bitcast.11), calls=%async_computation.4 | async-start | bytes 262144 | tf_op jit(solution)/shard_map/all_to_all | solution.py:81
  184.0 8.2 %all-to-all-done.4 = bf16[32,2,8,128]{3,2,1,0:T(8,128)(2,1)S(1)} async-done(((bf16[32,2,8,128]{3,2,1,0:T(8,128)(2,1)}), bf16[32,2,8,128]{3,2,1,0:T(8,128)(2,1)S(1)}, u32[]{:S(2)}, u32[]{:S(2)}) %all-to-all-start.4) | async-done | bytes 131104 | tf_op jit(solution)/shard_map/all_to_all | solution.py:81
  192.2 5.9 %while.45 = (s32[]{:T(128)}, f32[8,8,128]{2,0,1:T(8,128)S(1)}, s32[]{:T(128)}, s32[256]{0:T(256)}, s32[]{:T(128)}, /*index=5*/s32[256]{0:T(256)}, bf16[64,8,128]...) while((s32[]{:T(128)}, f32[8,8,128]{2,0,1:T(8,128)S(1)}, ...), condition=%wide.region_11.15_spmd.clone, body=%wide.region_10.14_spmd.clone.sunk | while | flops 23145028 | bytes 3086903 | solution.py:102
  192.2 1.4 compare_and_fusion.12
  194.2 2.8 %fusion.91 = f32[64,8,128]{2,1,0:T(8,128)S(1)} fusion(bf16[256,128,128]{2,1,0:T(8,128)(2,1)} %get-tuple-element.707, s32[]{:T(128)S(6)} %select_n.102, bf16[64,8,128]{2,1,0:T(8,128)(2,1)S(1)} %gather_fusion.3, pred[64]{0:T(512)(128)(4,1)S(1)} %get-tuple-element.566), kind=kOutput, calls=%fused_computation.54.clone.1 | convolution fusion | flops 16842752 | bytes 2490436 | tf_op jit(solution)/shard_map/while/body/gcf,gef->gce/dot_general | solution.py:91
  198.2 53.6 %all-reduce = (f32[8]{0:T(128)S(1)}, f32[8]{0:T(128)S(1)}) all-reduce(f32[8]{0:T(128)S(1)} %multiply_reduce_fusion.1, f32[8]{0:T(128)S(1)} %get-tuple-element.339), channel_id=1, replica_groups=mesh['rows'=32] {'rows'}, use_global_device_ids=true, to_apply=%region_13.17 | all-reduce | flops 16 | bytes 128 | tf_op jit(solution)/shard_map/psum | solution.py:18
  (50 shorter events, 16.7 us)
Async XLA Ops:
  3.2 17.5 %all-to-all-start = ((s32[32,1,2]{2,1,0:T(1,128)}), s32[32,1,2]{2,1,0:T(1,128)S(1)}, u32[]{:S(2)}, u32[]{:S(2)}) async-start(s32[32,1,2]{2,1,0:T(1,128)} %bitcast.1), calls=%async_computation | async-start | bytes 32768 | tf_op jit(solution)/shard_map/all_to_all | solution.py:46
  20.7 40.0 %all-to-all-start.1 = ((f32[32,2,8,128]{3,1,2,0:T(2,128)}), f32[32,2,8,128]{3,1,2,0:T(2,128)S(1)}, u32[]{:S(2)}, u32[]{:S(2)}) async-start(f32[32,2,8,128]{3,1,2,0:T(2,128)} %copy.29), calls=%async_computation.1 | async-start | bytes 524288 | tf_op jit(solution)/shard_map/all_to_all | solution.py:66
  62.5 10.8 %all-to-all-start.2 = ((bf16[32,2,8,128]{3,2,1,0:T(8,128)(2,1)}), bf16[32,2,8,128]{3,2,1,0:T(8,128)(2,1)S(1)}, u32[]{:S(2)}, u32[]{:S(2)}) async-start(bf16[32,2,8,128]{3,2,1,0:T(8,128)(2,1)} %bitcast.7), calls=%async_computation.2 | async-start | bytes 262144 | tf_op jit(solution)/shard_map/all_to_all | solution.py:81
  181.4 10.8 %all-to-all-start.4 = ((bf16[32,2,8,128]{3,2,1,0:T(8,128)(2,1)}), bf16[32,2,8,128]{3,2,1,0:T(8,128)(2,1)S(1)}, u32[]{:S(2)}, u32[]{:S(2)}) async-start(bf16[32,2,8,128]{3,2,1,0:T(8,128)(2,1)} %bitcast.11), calls=%async_computation.4 | async-start | bytes 262144 | tf_op jit(solution)/shard_map/all_to_all | solution.py:81
where the time goes:
time: 255 us; the launch traced here: 253 us
  blocking collectives  146 us (57%)
  starting transfers between devices  41.9 us (16%)
  waiting for transfers between devices  26.2 us (10%)
  other arithmetic  16 us (6%)
  matrix products  11.3 us (4%)
  local copies, waits for them, and re-layouts  10.7 us (4%)
    psum x2, blocking collectives, hub_norm_sum(): return lax.psum(square_sums(hub_raw), 'rows')  107 us
    all_to_all x1, blocking collectives, per_device(): lax.all_to_all(partial_value.reshape(devices, slots_each, columns, tile_e...  38.4 us
    all_to_all x1, starting transfers between devices, per_device(): lax.all_to_all(partial_value.reshape(devices, slots_each, columns, tile_e...  29.5 us
    all_to_all x2, waiting for transfers between devices, per_device(): lax.all_to_all(reply, 'rows', split_axis=0, concat_axis=0, tiled=True)  16.4 us
    all_to_all x1, waiting for transfers between devices, per_device(): lax.all_to_all(partial_value.reshape(devices, slots_each, columns, tile_e...  9.76 us
    all_to_all x1, starting transfers between devices, per_device(): lax.all_to_all(wanted_local.reshape(devices, slots_each), 'rows', split_a...  7.33 us
    dot_general x2, matrix products, forward_accumulate(): jnp.einsum('gcf,gef->gce', source, tiles_now, preferred_element_type=jnp....  5.59 us
    scatter-add x2, other arithmetic, transpose_accumulate(): jax.ops.segment_sum(product, slots_now, num_segments=slot_total)  5.5 us
  transfers between devices with their start and end apart: 4, of which 3 were waited for; matrix products, arithmetic and copies ran while one was open for 4% of the time, Pallas kernels for 0%

commit v1 on v0

v1 whole, which is shorter than its diff:
```python
import math

import jax
import jax.numpy as jnp
from jax import lax
from jax.experimental import pallas as pl
from jax.experimental.pallas import tpu as pltpu
from jax.sharding import PartitionSpec as P

ITERS = 2
EPS = 1e-06
GROUP = 8
CHUNK = 16
VMEM_LIMIT = 24 * 1024 * 1024

F32 = jnp.float32
BF16 = jnp.bfloat16


def tile_sweep(transposed, count, row_s, slot_s, tiles, source, accum, chunk, group, arrive):
    zero_at = source.shape[0] - 1
    columns, edge = source.shape[1:]
    half = group // 2
    pick, put = (row_s, slot_s) if transposed else (slot_s, row_s)

    def one_group(base):
        blocks = []
        targets = []
        for t in range(group):
            at = base + t
            blocks.append(source[jnp.where(at < count, pick[at], zero_at)])
            targets.append(put[at])
        pad = jnp.zeros((columns * half, edge), F32)
        left = jnp.concatenate(
            [
                jnp.concatenate(blocks[0::2] + [pad], 0),
                jnp.concatenate([pad] + blocks[1::2], 0),
            ],
            1,
        ).astype(BF16)
        weights = [tiles[base + t] for t in range(group)]
        outer, inner = (1, 0) if transposed else (0, 1)
        right = jnp.concatenate(
            [jnp.concatenate(weights[0::2], outer), jnp.concatenate(weights[1::2], outer)], inner
        )
        product = lax.dot_general(
            left, right, (((1,), (inner,)), ((), ())), preferred_element_type=F32
        )
        for t in range(group):
            first = (t % 2) * columns * half + (t // 2) * columns
            lane = (t // 2) * edge
            accum[targets[t]] += product[first : first + columns, lane : lane + edge]

    def one_chunk(c, carry):
        arrive(c)

        def two_groups(g, inner_carry):
            base = c * chunk + g * 2 * group
            one_group(base)
            one_group(base + group)
            return inner_carry

        return lax.fori_loop(0, chunk // (2 * group), two_groups, carry)

    lax.fori_loop(0, (count + chunk - 1) // chunk, one_chunk, 0)


def pack_blocks(accum, send, devices, slots_each):
    columns = accum.shape[1]
    for p in range(devices):
        both = jnp.concatenate([accum[p * slots_each + k] for k in range(slots_each)], 0)
        send[p, : slots_each * columns, :] = both.astype(BF16)


def solution(mesh):
    devices = mesh.shape["rows"]

    def per_device(edge_tiles, tile_row, tile_slot, tile_count, fetch_list, hub_start):
        tile_total, edge, _ = edge_tiles.shape
        columns = hub_start.shape[0]
        blocks = hub_start.shape[1] // edge
        slot_total = fetch_list.shape[1]
        slots_each = slot_total // devices
        node_total = hub_start.shape[1] * devices
        chunk = math.gcd(CHUNK, tile_total)
        group = min(GROUP, chunk // 2)
        rows_each = slots_each * columns
        assert blocks**slots_each <= 256 and group % 2 == 0

        smem = pl.BlockSpec(memory_space=pltpu.SMEM)
        vmem = pl.BlockSpec(memory_space=pltpu.VMEM)
        hbm = pl.BlockSpec(memory_space=pltpu.HBM)
        params = pltpu.CompilerParams(vmem_limit_bytes=VMEM_LIMIT)

        def start_kernel(cnt, row_s, slot_s, fetch, hub, tiles, send, kept, source, accum, sems):
            count = cnt[0]

            def copy(c):
                span = pl.ds(c * chunk, chunk)
                return pltpu.make_async_copy(tiles.at[span], kept.at[span], sems.at[c])

            def begin(c, carry):
                copy(c).start()
                return carry

            lax.fori_loop(0, (count + chunk - 1) // chunk, begin, 0)
            for b in range(blocks):
                source[b] = hub[:, b * edge : (b + 1) * edge].astype(BF16).astype(F32)
            source[blocks] = jnp.zeros((columns, edge), F32)
            accum[...] = jnp.zeros_like(accum)
            tile_sweep(
                True, count, row_s, slot_s, kept, source, accum, chunk, group,
                lambda c: copy(c).wait(),
            )
            pack_blocks(accum, send, devices, slots_each)
            for p in range(devices):
                code = fetch[0, p * slots_each]
                for k in range(1, slots_each):
                    code = code + fetch[0, p * slots_each + k] * blocks**k
                send[p, rows_each:, :] = jnp.full((columns, edge), code, jnp.int32).astype(F32).astype(BF16)

        def owner_kernel(got, codes, raw, reply, squares):
            totals = [jnp.zeros((columns, edge), F32) for _ in range(blocks)]

            def entries(p):
                code = codes[p, rows_each:, :].astype(F32)
                wanted = []
                for k in range(slots_each - 1, 0, -1):
                    high = jnp.floor(code * (1.0 / blocks**k))
                    wanted.append(high)
                    code = code - high * blocks**k
                return (wanted + [code])[::-1]

            for p in range(devices):
                wanted = entries(p)
                values = got[p, :rows_each, :].astype(F32)
                for k in range(slots_each):
                    value = values[k * columns : (k + 1) * columns]
                    for b in range(blocks):
                        totals[b] = totals[b] + jnp.where(wanted[k] == b, value, 0.0)
            square = jnp.zeros((columns, edge), F32)
            for b in range(blocks):
                raw[:, b * edge : (b + 1) * edge] = totals[b]
                square = square + totals[b] * totals[b]
            squares[...] = square
            for p in range(devices):
                wanted = entries(p)
                out = []
                for k in range(slots_each):
                    chosen = totals[0]
                    for b in range(1, blocks):
                        chosen = jnp.where(wanted[k] == b, totals[b], chosen)
                    out.append(chosen)
                reply[p] = jnp.concatenate(out, 0).astype(BF16)

        def load_fetched(fetched, source):
            for p in range(devices):
                both = fetched[p].astype(F32)
                for k in range(slots_each):
                    source[p * slots_each + k] = both[k * columns : (k + 1) * columns]
            source[slot_total] = jnp.zeros((columns, edge), F32)

        def middle_kernel(cnt, row_s, slot_s, fetched, tiles, send, squares, source, hub, accum, low):
            count = cnt[0]
            load_fetched(fetched, source)
            hub[...] = jnp.zeros_like(hub)
            accum[...] = jnp.zeros_like(accum)
            tile_sweep(
                False, count, row_s, slot_s, tiles, source, hub, chunk, group, lambda c: None
            )
            square = jnp.zeros((columns, edge), F32)
            for b in range(blocks):
                value = hub[b]
                square = square + value * value
                low[b] = value.astype(BF16).astype(F32)
            low[blocks] = jnp.zeros((columns, edge), F32)
            squares[...] = square
            tile_sweep(
                True, count, row_s, slot_s, tiles, low, accum, chunk, group, lambda c: None
            )
            pack_blocks(accum, send, devices, slots_each)

        def last_kernel(cnt, row_s, slot_s, fetched, tiles, first_squares, authority_squares, raw, send, source, hub):
            count = cnt[0]
            load_fetched(fetched, source)
            hub[...] = jnp.zeros_like(hub)
            tile_sweep(
                False, count, row_s, slot_s, tiles, source, hub, chunk, group, lambda c: None
            )
            largest = jnp.zeros((columns, edge), F32)
            for b in range(blocks):
                largest = jnp.maximum(largest, jnp.abs(hub[b]))
            peak = jnp.max(largest, axis=1, keepdims=True)
            inverse = jnp.where(peak > 1e-30, 1.0 / jnp.maximum(peak, 1e-30), 0.0)
            square = jnp.zeros((columns, edge), F32)
            for b in range(blocks):
                value = hub[b]
                raw[:, b * edge : (b + 1) * edge] = value
                scaled = value * inverse
                square = square + scaled * scaled
            stats = [
                jnp.sum(first_squares[...], axis=1, keepdims=True),
                jnp.sum(authority_squares[...], axis=1, keepdims=True),
                jnp.sum(square, axis=1, keepdims=True),
                peak,
            ]
            lane = lax.broadcasted_iota(jnp.int32, (columns, edge), 1)
            sub = lax.broadcasted_iota(jnp.int32, (columns, edge), 0)
            mixed = jnp.zeros((columns, edge), F32)
            for j, stat in enumerate(stats):
                mixed = jnp.where(lane == sub + j * columns, stat, mixed)
            line = jnp.sum(mixed, axis=0, keepdims=True)
            send[...] = jnp.broadcast_to(line, send.shape)

        def finish_kernel(got, hub_raw, authority_raw, hub, authority):
            rows = got[...]
            lane = lax.broadcasted_iota(jnp.int32, (columns, edge), 1)
            sub = lax.broadcasted_iota(jnp.int32, (columns, edge), 0)

            def column(line, j):
                spread = jnp.broadcast_to(line, (columns, edge))
                kept = jnp.where(lane == sub + j * columns, spread, 0.0)
                return jnp.sum(kept, axis=1, keepdims=True)

            sums = jnp.sum(rows, axis=0, keepdims=True)
            first = column(sums, 0) / node_total
            first_scale = 1.0 / jnp.sqrt(first + EPS)
            authority_mean = column(sums, 1) / node_total * first_scale * first_scale
            at_peaks = jnp.sum(
                jnp.where(lane == sub + 3 * columns, first_scale, 0.0), axis=0, keepdims=True
            )
            peaks = rows * at_peaks
            peaks = pltpu.roll(peaks, edge - columns, 1)
            hub_sums = jnp.sum(rows * (peaks * peaks), axis=0, keepdims=True)
            hub_mean = column(hub_sums, 2) / node_total
            authority[...] = authority_raw[...] * (
                first_scale / jnp.sqrt(authority_mean + EPS)
            )
            hub[...] = hub_raw[...] * (first_scale / jnp.sqrt(hub_mean + EPS))

        def shape(dims, kind):
            return jax.ShapeDtypeStruct(dims, kind)

        block_shape = (columns, edge)
        source_blocks = pltpu.VMEM((blocks + 1,) + block_shape, F32)
        source_slots = pltpu.VMEM((slot_total + 1,) + block_shape, F32)
        sum_blocks = pltpu.VMEM((blocks,) + block_shape, F32)
        sum_slots = pltpu.VMEM((slot_total,) + block_shape, F32)
        whole = shape((columns, blocks * edge), F32)
        plain = shape((devices, rows_each, edge), BF16)
        square_shape = shape(block_shape, F32)

        def exchange(value):
            return lax.all_to_all(value, "rows", split_axis=0, concat_axis=0, tiled=True)

        send, tiles = pl.pallas_call(
            start_kernel,
            name="start",
            out_shape=(
                shape((devices, rows_each + columns, edge), BF16),
                shape(edge_tiles.shape, edge_tiles.dtype),
            ),
            in_specs=[smem, smem, smem, smem, vmem, hbm],
            out_specs=(vmem, vmem),
            scratch_shapes=[source_blocks, sum_slots, pltpu.SemaphoreType.DMA((tile_total // chunk,))],
            compiler_params=params,
        )(
            tile_count, tile_row, tile_slot, fetch_list, hub_start,
            pltpu.with_memory_space_constraint(edge_tiles, pltpu.HBM),
        )
        first = exchange(send)

        def owner(got):
            return pl.pallas_call(
                owner_kernel,
                name="owner",
                out_shape=(whole, plain, square_shape),
                in_specs=[vmem, vmem],
                out_specs=(vmem, vmem, vmem),
                compiler_params=params,
            )(got, first)

        _, reply, _ = owner(first)
        send, first_squares = pl.pallas_call(
            middle_kernel,
            name="middle",
            out_shape=(plain, square_shape),
            in_specs=[smem, smem, smem, vmem, vmem],
            out_specs=(vmem, vmem),
            scratch_shapes=[source_slots, sum_blocks, sum_slots, source_blocks],
            compiler_params=params,
        )(tile_count, tile_row, tile_slot, exchange(reply), tiles)
        authority_raw, reply, authority_squares = owner(exchange(send))
        hub_raw, send = pl.pallas_call(
            last_kernel,
            name="last",
            out_shape=(whole, shape((devices, edge), F32)),
            in_specs=[smem, smem, smem, vmem, vmem, vmem, vmem],
            out_specs=(vmem, vmem),
            scratch_shapes=[source_slots, sum_blocks],
            compiler_params=params,
        )(tile_count, tile_row, tile_slot, exchange(reply), tiles, first_squares, authority_squares)
        return pl.pallas_call(
            finish_kernel,
            name="finish",
            out_shape=(whole, whole),
            in_specs=[vmem, vmem, vmem],
            out_specs=(vmem, vmem),
            compiler_params=params,
        )(exchange(send), hub_raw, authority_raw)

    in_specs = (
        P("rows", None, None),
        P("rows"),
        P("rows"),
        P("rows"),
        P("rows", None),
        P(None, "rows"),
    )
    out_specs = (P(None, "rows"), P(None, "rows"))
    return jax.shard_map(
        per_device, mesh=mesh, in_specs=in_specs, out_specs=out_specs, check_vma=False
    )
```

time: 255 us -> 82.4 us (0.32)
  blocking collectives: 146 us -> 69.5 us
  starting transfers between devices: 41.9 us -> 0 us
  waiting for transfers between devices: 26.2 us -> 0 us
  other arithmetic: 16 us -> 0 us
  matrix products: 11.3 us -> 0 us
  local copies, waits for them, and re-layouts: 10.7 us -> 2.77 us
  Pallas kernels: 0 us -> 7.51 us
    psum x2 -> x0, blocking collectives: 107 us -> none  [hub_norm_sum(): return lax.psum(square_sums(hub_raw), 'rows')]
    all_to_all x4 -> x0, starting transfers between devices: 41.9 us -> none  [the longest x1 29.5 us: per_device(): lax.all_to_all(partial_value.reshape(devices, slots_each, columns, tile_e...]
    all_to_all x1 -> x5, blocking collectives: 38.4 us -> 69.5 us  [exchange(): lax.all_to_all(value, 'rows', split_axis=0, concat_axis=0, tiled=True)]
    all_to_all x4 -> x0, waiting for transfers between devices: 26.2 us -> none  [the longest x2 16.4 us: per_device(): lax.all_to_all(reply, 'rows', split_axis=0, concat_axis=0, tiled=True)]
    dot_general x8 -> x0, matrix products: 11.3 us -> none  [the longest x2 5.59 us: forward_accumulate(): jnp.einsum('gcf,gef->gce', source, tiles_now, preferred_element_type=jnp....]
    pallas_call x0 -> x6, Pallas kernels: none -> 7.51 us  [the longest x1 2.27 us: per_device(): pl.pallas_call(start_kernel, name='start', out_shape=(shape((devices, row...]
    and x5 -> x0, other arithmetic: 5.63 us -> none  [the longest x2 2.81 us: transpose_accumulate(): source = jnp.take(hub_low, rows_now, axis=0)]
    scatter-add x2 -> x0, other arithmetic: 5.5 us -> none  [transpose_accumulate(): jax.ops.segment_sum(product, slots_now, num_segments=slot_total)]
  transfers between devices with their start and end apart: 4 -> 0, of which waited for: 3 -> 0; matrix products, arithmetic and copies ran while one was open for 4% -> 0% of each run, Pallas kernels for 0% -> 0%
where the time goes in v1:
time: 82.4 us; the launch traced here: 81.1 us
  blocking collectives  69.5 us (84%)
  Pallas kernels  7.51 us (9%)
  local copies, waits for them, and re-layouts  2.77 us (3%)
  between operations  1.31 us (2%)
    all_to_all x5, blocking collectives, exchange(): lax.all_to_all(value, 'rows', split_axis=0, concat_axis=0, tiled=True)  69.5 us
    unnamed x12, local copies, waits for them, and re-layouts  2.77 us
    pallas_call x1, Pallas kernels, per_device(): pl.pallas_call(start_kernel, name='start', out_shape=(shape((devices, row...  2.27 us
    pallas_call x1, Pallas kernels, per_device(): pl.pallas_call(middle_kernel, name='middle', out_shape=(plain, square_sha...  1.69 us

profile of v1, /device:TPU:0, one launch (start us, length us, event | category | flops | bytes accessed | tf_op | source)
XLA Modules:
  0.0 81.1 jit_solution(13257275020278198350)
XLA Ops:
  1.3 0.0 copy-start
  1.3 0.7 copy-done
  2.0 0.0 copy-start.1
  2.0 0.7 copy-done.1
  2.7 0.0 copy-start.3
  2.7 0.7 copy-done.3
  3.4 0.0 copy-start.5
  3.4 0.7 copy-done.5
  4.1 0.0 copy-start.2
  4.1 0.0 copy-start.4
  4.1 2.3 %start.1 = (bf16[32,24,128]{2,1,0:T(8,128)(2,1)S(1)}, bf16[256,128,128]{2,1,0:T(8,128)(2,1)S(1)}) custom-call(s32[1]{0:T(128)S(6)} %copy.9.cnt, s32[256]{0:T(256)S(1)} %copy-done.1, s32[256]{0:T(256)S(1)} %copy-done.3, s32[1,64]{1,0:T(1,128)S(1)} %copy-done.5, f32[8,1024]{1,0:T(8,128)S(1)} %copy-done, bf16[256,128,128]{2,1,0:T(8,128)(2,1)} %tiles.1), custom_call_target="tpu_custom_call" | custom-call | tf_op jit(solution)/shard_map/start/pallas_call | solution.py:256
  6.3 19.1 %all_to_all.31.got.codes = bf16[32,24,128]{2,1,0:T(8,128)(2,1)S(1)} all-to-all(bf16[32,24,128]{2,1,0:T(8,128)(2,1)S(1)} %get-tuple-element.12), channel_id=1, replica_groups=mesh['rows'=32] {'rows'}, dimensions={0} | all-to-all | bytes 393216 | tf_op jit(solution)/shard_map/all_to_all | solution.py:254
  25.5 0.9 %owner.2 = (f32[8,1024]{1,0:T(8,128)}, bf16[32,16,128]{2,1,0:T(8,128)(2,1)S(1)}, f32[8,128]{1,0:T(8,128)}) custom-call(bf16[32,24,128]{2,1,0:T(8,128)(2,1)S(1)} %all_to_all.31.got.codes, bf16[32,24,128]{2,1,0:T(8,128)(2,1)S(1)} %all_to_all.31.got.codes), custom_call_target="tpu_custom_call" | custom-call | tf_op jit(solution)/shard_map/owner/pallas_call | solution.py:274
  26.4 10.6 %all_to_all.32.fetched = bf16[32,16,128]{2,1,0:T(8,128)(2,1)S(1)} all-to-all(bf16[32,16,128]{2,1,0:T(8,128)(2,1)S(1)} %get-tuple-element.13), channel_id=1, replica_groups=mesh['rows'=32] {'rows'}, dimensions={0} | all-to-all | bytes 262144 | tf_op jit(solution)/shard_map/all_to_all | solution.py:254
  37.0 1.7 %middle.1 = (bf16[32,16,128]{2,1,0:T(8,128)(2,1)S(1)}, f32[8,128]{1,0:T(8,128)S(1)}) custom-call(s32[1]{0:T(128)S(6)} %copy.9.cnt, s32[256]{0:T(256)S(1)} %copy-done.1, s32[256]{0:T(256)S(1)} %copy-done.3, bf16[32,16,128]{2,1,0:T(8,128)(2,1)S(1)} %all_to_all.32.fetched, bf16[256,128,128]{2,1,0:T(8,128)(2,1)S(1)} %get-tuple-element.14.tiles), custom_call_target="tpu_custom_call" | custom-call | tf_op jit(solution)/shard_map/middle/pallas_call | solution.py:284
  38.7 17.0 %all_to_all.33.got = bf16[32,16,128]{2,1,0:T(8,128)(2,1)S(1)} all-to-all(bf16[32,16,128]{2,1,0:T(8,128)(2,1)S(1)} %get-tuple-element.15), channel_id=1, replica_groups=mesh['rows'=32] {'rows'}, dimensions={0} | all-to-all | bytes 262144 | tf_op jit(solution)/shard_map/all_to_all | solution.py:254
  55.7 0.4 owner.3
  56.0 10.0 %all_to_all.34.fetched = bf16[32,16,128]{2,1,0:T(8,128)(2,1)S(1)} all-to-all(bf16[32,16,128]{2,1,0:T(8,128)(2,1)S(1)} %get-tuple-element.16), channel_id=1, replica_groups=mesh['rows'=32] {'rows'}, dimensions={0} | all-to-all | bytes 262144 | tf_op jit(solution)/shard_map/all_to_all | solution.py:254
  66.0 0.0 copy-done.2
  66.0 0.0 copy-done.4
  66.0 1.4 %last.1 = (f32[8,1024]{1,0:T(8,128)S(1)}, f32[32,128]{1,0:T(8,128)S(1)}) custom-call(s32[1]{0:T(128)S(6)} %copy.9.cnt, s32[256]{0:T(256)S(1)} %copy-done.2, s32[256]{0:T(256)S(1)} %copy-done.4, bf16[32,16,128]{2,1,0:T(8,128)(2,1)S(1)} %all_to_all.34.fetched, bf16[256,128,128]{2,1,0:T(8,128)(2,1)S(1)} %get-tuple-element.14.tiles, ...), custom_call_target="tpu_custom_call" | custom-call | tf_op jit(solution)/shard_map/last/pallas_call | solution.py:294
  67.4 12.8 %all_to_all.35 = f32[32,1,128]{2,1,0:T(1,128)S(1)} all-to-all(f32[32,1,128]{2,1,0:T(1,128)S(1)} %bitcast.5), channel_id=1, replica_groups=mesh['rows'=32] {'rows'}, dimensions={0} | all-to-all | bytes 32768 | tf_op jit(solution)/shard_map/all_to_all | solution.py:254
  80.2 0.9 %finish.1 = (f32[8,1024]{1,0:T(8,128)}, f32[8,1024]{1,0:T(8,128)}) custom-call(f32[32,128]{1,0:T(8,128)S(1)} %bitcast.4, f32[8,1024]{1,0:T(8,128)S(1)} %get-tuple-element.20.hub_raw, f32[8,1024]{1,0:T(8,128)S(1)} %get-tuple-element.21.authority_raw), custom_call_target="tpu_custom_call" | custom-call | tf_op jit(solution)/shard_map/finish/pallas_call | solution.py:303
Async XLA Ops:
  1.3 0.8 copy-start
  2.0 0.7 copy-start.1
  2.7 0.7 copy-start.3
  3.4 0.7 copy-start.5
  4.1 62.0 %copy-start.2 = (s32[256]{0:T(256)S(1)}, s32[256]{0:T(256)}, u32[]{:S(2)}) copy-start(s32[256]{0:T(256)} %row_s.5) | copy-start | bytes 3076
  4.1 62.0 %copy-start.4 = (s32[256]{0:T(256)S(1)}, s32[256]{0:T(256)}, u32[]{:S(2)}) copy-start(s32[256]{0:T(256)} %slot_s.5) | copy-start | bytes 3076

commit v2 on v1

--- a/solution.py
+++ b/solution.py
@@ -10,7 +10,8 @@
 ITERS = 2
 EPS = 1e-06
 GROUP = 8
-CHUNK = 16
+COPY_TILES = 32
+STEP_TILES = 64
 VMEM_LIMIT = 24 * 1024 * 1024
 
 F32 = jnp.float32
@@ -54,13 +55,9 @@
     def one_chunk(c, carry):
         arrive(c)
 
-        def two_groups(g, inner_carry):
-            base = c * chunk + g * 2 * group
-            one_group(base)
-            one_group(base + group)
-            return inner_carry
-
-        return lax.fori_loop(0, chunk // (2 * group), two_groups, carry)
+        for g in range(chunk // group):
+            one_group(c * chunk + g * group)
+        return carry
 
     lax.fori_loop(0, (count + chunk - 1) // chunk, one_chunk, 0)
 
@@ -82,8 +79,10 @@
         slot_total = fetch_list.shape[1]
         slots_each = slot_total // devices
         node_total = hub_start.shape[1] * devices
-        chunk = math.gcd(CHUNK, tile_total)
-        group = min(GROUP, chunk // 2)
+        chunk = math.gcd(COPY_TILES, tile_total)
+        step = math.gcd(STEP_TILES, tile_total)
+        group = math.gcd(GROUP, chunk)
+        always = min(2, tile_total // chunk)
         rows_each = slots_each * columns
         assert blocks**slots_each <= 256 and group % 2 == 0
 
@@ -92,9 +91,10 @@
         hbm = pl.BlockSpec(memory_space=pltpu.HBM)
         params = pltpu.CompilerParams(vmem_limit_bytes=VMEM_LIMIT)
 
-        def start_kernel(cnt, row_s, slot_s, fetch, hub, tiles, send, kept, source, accum, sems):
-            count = cnt[0]
-
+        def start_kernel(
+            cnt, row_hbm, slot_hbm, fetch_hbm, hub_hbm, tiles,
+            send, kept, row_s, slot_s, fetch, hub, source, accum, sems, small
+        ):
             def copy(c):
                 span = pl.ds(c * chunk, chunk)
                 return pltpu.make_async_copy(tiles.at[span], kept.at[span], sems.at[c])
@@ -103,23 +103,40 @@
                 copy(c).start()
                 return carry
 
-            lax.fori_loop(0, (count + chunk - 1) // chunk, begin, 0)
+            def end(c, carry):
+                copy(c).wait()
+                return carry
+
+            pairs = [(hub_hbm, hub), (row_hbm, row_s), (slot_hbm, slot_s), (fetch_hbm, fetch)]
+            parts = [pltpu.make_async_copy(a, b, small.at[i]) for i, (a, b) in enumerate(pairs)]
+            for part in parts:
+                part.start()
+            for c in range(always):
+                copy(c).start()
+            accum[...] = jnp.zeros_like(accum)
+            source[blocks] = jnp.zeros((columns, edge), F32)
+            count = cnt[0]
+            live = (count + chunk - 1) // chunk
+            lax.fori_loop(always, live, begin, 0)
+            for part in parts:
+                part.wait()
             for b in range(blocks):
                 source[b] = hub[:, b * edge : (b + 1) * edge].astype(BF16).astype(F32)
-            source[blocks] = jnp.zeros((columns, edge), F32)
-            accum[...] = jnp.zeros_like(accum)
             tile_sweep(
                 True, count, row_s, slot_s, kept, source, accum, chunk, group,
                 lambda c: copy(c).wait(),
             )
+            lax.fori_loop(live, always, end, 0)
             pack_blocks(accum, send, devices, slots_each)
             for p in range(devices):
                 code = fetch[0, p * slots_each]
                 for k in range(1, slots_each):
                     code = code + fetch[0, p * slots_each + k] * blocks**k
-                send[p, rows_each:, :] = jnp.full((columns, edge), code, jnp.int32).astype(F32).astype(BF16)
-
-        def owner_kernel(got, codes, raw, reply, squares):
+                send[p, rows_each:, :] = (
+                    jnp.full((columns, edge), code, jnp.int32).astype(F32).astype(BF16)
+                )
+
+        def owner_kernel(got, codes, reply, raw=None, squares=None):
             totals = [jnp.zeros((columns, edge), F32) for _ in range(blocks)]
 
             def entries(p):
@@ -138,11 +155,12 @@
                     value = values[k * columns : (k + 1) * columns]
                     for b in range(blocks):
                         totals[b] = totals[b] + jnp.where(wanted[k] == b, value, 0.0)
-            square = jnp.zeros((columns, edge), F32)
-            for b in range(blocks):
-                raw[:, b * edge : (b + 1) * edge] = totals[b]
-                square = square + totals[b] * totals[b]
-            squares[...] = square
+            if raw is not None:
+                square = jnp.zeros((columns, edge), F32)
+                for b in range(blocks):
+                    raw[:, b * edge : (b + 1) * edge] = totals[b]
+                    square = square + totals[b] * totals[b]
+                squares[...] = square
             for p in range(devices):
                 wanted = entries(p)
                 out = []
@@ -166,7 +184,7 @@
             hub[...] = jnp.zeros_like(hub)
             accum[...] = jnp.zeros_like(accum)
             tile_sweep(
-                False, count, row_s, slot_s, tiles, source, hub, chunk, group, lambda c: None
+                False, count, row_s, slot_s, tiles, source, hub, step, group, lambda c: None
             )
             square = jnp.zeros((columns, edge), F32)
             for b in range(blocks):
@@ -176,7 +194,7 @@
             low[blocks] = jnp.zeros((columns, edge), F32)
             squares[...] = square
             tile_sweep(
-                True, count, row_s, slot_s, tiles, low, accum, chunk, group, lambda c: None
+                True, count, row_s, slot_s, tiles, low, accum, step, group, lambda c: None
             )
             pack_blocks(accum, send, devices, slots_each)
 
@@ -185,7 +203,7 @@
             load_fetched(fetched, source)
             hub[...] = jnp.zeros_like(hub)
             tile_sweep(
-                False, count, row_s, slot_s, tiles, source, hub, chunk, group, lambda c: None
+                False, count, row_s, slot_s, tiles, source, hub, step, group, lambda c: None
             )
             largest = jnp.zeros((columns, edge), F32)
             for b in range(blocks):
@@ -253,6 +271,8 @@
         def exchange(value):
             return lax.all_to_all(value, "rows", split_axis=0, concat_axis=0, tiled=True)
 
+        small = [tile_count, tile_row, tile_slot]
+        operands = small + [fetch_list, hub_start, edge_tiles]
         send, tiles = pl.pallas_call(
             start_kernel,
             name="start",
@@ -260,27 +280,32 @@
                 shape((devices, rows_each + columns, edge), BF16),
                 shape(edge_tiles.shape, edge_tiles.dtype),
             ),
-            in_specs=[smem, smem, smem, smem, vmem, hbm],
+            in_specs=[smem] + [hbm] * 5,
             out_specs=(vmem, vmem),
-            scratch_shapes=[source_blocks, sum_slots, pltpu.SemaphoreType.DMA((tile_total // chunk,))],
+            scratch_shapes=[
+                *[pltpu.SMEM(a.shape, a.dtype) for a in small[1:]],
+                pltpu.SMEM(fetch_list.shape, fetch_list.dtype),
+                pltpu.VMEM(hub_start.shape, F32),
+                source_blocks,
+                sum_slots,
+                pltpu.SemaphoreType.DMA((tile_total // chunk,)),
+                pltpu.SemaphoreType.DMA((4,)),
+            ],
             compiler_params=params,
-        )(
-            tile_count, tile_row, tile_slot, fetch_list, hub_start,
-            pltpu.with_memory_space_constraint(edge_tiles, pltpu.HBM),
-        )
+        )(tile_count, *[pltpu.with_memory_space_constraint(a, pltpu.HBM) for a in operands[1:]])
         first = exchange(send)
 
-        def owner(got):
+        def owner(got, outputs):
             return pl.pallas_call(
                 owner_kernel,
                 name="owner",
-                out_shape=(whole, plain, square_shape),
+                out_shape=(plain, whole, square_shape)[:outputs],
                 in_specs=[vmem, vmem],
-                out_specs=(vmem, vmem, vmem),
+                out_specs=(vmem, vmem, vmem)[:outputs],
                 compiler_params=params,
             )(got, first)
 
-        _, reply, _ = owner(first)
+        (reply,) = owner(first, 1)
         send, first_squares = pl.pallas_call(
             middle_kernel,
             name="middle",
@@ -289,8 +314,8 @@
             out_specs=(vmem, vmem),
             scratch_shapes=[source_slots, sum_blocks, sum_slots, source_blocks],
             compiler_params=params,
-        )(tile_count, tile_row, tile_slot, exchange(reply), tiles)
-        authority_raw, reply, authority_squares = owner(exchange(send))
+        )(*small, exchange(reply), tiles)
+        reply, authority_raw, authority_squares = owner(exchange(send), 3)
         hub_raw, send = pl.pallas_call(
             last_kernel,
             name="last",
@@ -299,7 +324,7 @@
             out_specs=(vmem, vmem),
             scratch_shapes=[source_slots, sum_blocks],
             compiler_params=params,
-        )(tile_count, tile_row, tile_slot, exchange(reply), tiles, first_squares, authority_squares)
+        )(*small, exchange(reply), tiles, first_squares, authority_squares)
         return pl.pallas_call(
             finish_kernel,
             name="finish",

time: 82.4 us -> 72.6 us (0.88); the launches traced: 81.1 us -> 72.4 us
  blocking collectives: 69.5 us -> 64.2 us
  local copies, waits for them, and re-layouts: 2.77 us -> 0.01 us
    all_to_all x5, blocking collectives: 69.5 us -> 64.2 us  [exchange(): lax.all_to_all(value, 'rows', split_axis=0, concat_axis=0, tiled=True)]
    unnamed x12 -> x4, local copies, waits for them, and re-layouts: 2.77 us -> 0.01 us
where the time goes in v2:
time: 72.6 us; the launch traced here: 72.4 us
  blocking collectives  64.2 us (88%)
  Pallas kernels  6.87 us (9%)
  between operations  1.34 us (2%)
    all_to_all x5, blocking collectives, exchange(): lax.all_to_all(value, 'rows', split_axis=0, concat_axis=0, tiled=True)  64.2 us
    pallas_call x1, Pallas kernels, per_device(): pl.pallas_call(middle_kernel, name='middle', out_shape=(plain, square_sha...  1.92 us
    pallas_call x1, Pallas kernels, per_device(): pl.pallas_call(start_kernel, name='start', out_shape=(shape((devices, row...  1.74 us
    pallas_call x1, Pallas kernels, per_device(): pl.pallas_call(last_kernel, name='last', out_shape=(whole, shape((devices...  1.55 us

profile of v2, /device:TPU:0, one launch (start us, length us, event | category | flops | bytes accessed | tf_op | source)
XLA Modules:
  0.0 72.4 jit_solution(17840489321069600237)
XLA Ops:
  0.6 0.0 copy-start.1
  0.6 0.0 copy-start
  1.3 1.7 %start.1 = (bf16[32,24,128]{2,1,0:T(8,128)(2,1)S(1)}, bf16[256,128,128]{2,1,0:T(8,128)(2,1)S(1)}) custom-call(s32[1]{0:T(128)S(6)} %copy.9.cnt, s32[256]{0:T(256)} %row_s.3, s32[256]{0:T(256)} %slot_s.3, s32[1,64]{1,0:T(1,128)} %fetch_hbm.1, f32[8,1024]{1,0:T(8,128)} %hub_hbm.1, bf16[256,128,128]{2,1,0:T(8,128)(2,1)} %tiles.1), custom_call_target="tpu_custom_call" | custom-call | tf_op jit(solution)/shard_map/start/pallas_call | solution.py:276
  3.1 18.4 %all_to_all.31.got.codes = bf16[32,24,128]{2,1,0:T(8,128)(2,1)S(1)} all-to-all(bf16[32,24,128]{2,1,0:T(8,128)(2,1)S(1)} %get-tuple-element.11), channel_id=1, replica_groups=mesh['rows'=32] {'rows'}, dimensions={0} | all-to-all | bytes 393216 | tf_op jit(solution)/shard_map/all_to_all | solution.py:272
  21.5 0.4 owner.2
  21.9 10.6 %all_to_all.32.fetched = bf16[32,16,128]{2,1,0:T(8,128)(2,1)S(1)} all-to-all(bf16[32,16,128]{2,1,0:T(8,128)(2,1)S(1)} %owner.2), channel_id=1, replica_groups=mesh['rows'=32] {'rows'}, dimensions={0} | all-to-all | bytes 262144 | tf_op jit(solution)/shard_map/all_to_all | solution.py:272
  32.5 0.0 copy-done.1
  32.5 0.0 copy-done
  32.5 1.9 %middle.1 = (bf16[32,16,128]{2,1,0:T(8,128)(2,1)S(1)}, f32[8,128]{1,0:T(8,128)S(1)}) custom-call(s32[1]{0:T(128)S(6)} %copy.9.cnt, s32[256]{0:T(256)S(1)} %copy-done, s32[256]{0:T(256)S(1)} %copy-done.1, bf16[32,16,128]{2,1,0:T(8,128)(2,1)S(1)} %all_to_all.32.fetched, bf16[256,128,128]{2,1,0:T(8,128)(2,1)S(1)} %get-tuple-element.12.tiles), custom_call_target="tpu_custom_call" | custom-call | tf_op jit(solution)/shard_map/middle/pallas_call | solution.py:309
  34.4 13.8 %all_to_all.33.got = bf16[32,16,128]{2,1,0:T(8,128)(2,1)S(1)} all-to-all(bf16[32,16,128]{2,1,0:T(8,128)(2,1)S(1)} %get-tuple-element.13), channel_id=1, replica_groups=mesh['rows'=32] {'rows'}, dimensions={0} | all-to-all | bytes 262144 | tf_op jit(solution)/shard_map/all_to_all | solution.py:272
  48.3 0.4 owner.3
  48.7 10.0 %all_to_all.34.fetched = bf16[32,16,128]{2,1,0:T(8,128)(2,1)S(1)} all-to-all(bf16[32,16,128]{2,1,0:T(8,128)(2,1)S(1)} %get-tuple-element.14), channel_id=1, replica_groups=mesh['rows'=32] {'rows'}, dimensions={0} | all-to-all | bytes 262144 | tf_op jit(solution)/shard_map/all_to_all | solution.py:272
  58.6 1.5 %last.1 = (f32[8,1024]{1,0:T(8,128)S(1)}, f32[32,128]{1,0:T(8,128)S(1)}) custom-call(s32[1]{0:T(128)S(6)} %copy.9.cnt, s32[256]{0:T(256)S(1)} %copy-done, s32[256]{0:T(256)S(1)} %copy-done.1, bf16[32,16,128]{2,1,0:T(8,128)(2,1)S(1)} %all_to_all.34.fetched, bf16[256,128,128]{2,1,0:T(8,128)(2,1)S(1)} %get-tuple-element.12.tiles, ...), custom_call_target="tpu_custom_call" | custom-call | tf_op jit(solution)/shard_map/last/pallas_call | solution.py:319
  60.2 11.3 %all_to_all.35 = f32[32,1,128]{2,1,0:T(1,128)S(1)} all-to-all(f32[32,1,128]{2,1,0:T(1,128)S(1)} %bitcast.5), channel_id=1, replica_groups=mesh['rows'=32] {'rows'}, dimensions={0} | all-to-all | bytes 32768 | tf_op jit(solution)/shard_map/all_to_all | solution.py:272
  71.5 0.9 %finish.1 = (f32[8,1024]{1,0:T(8,128)}, f32[8,1024]{1,0:T(8,128)}) custom-call(f32[32,128]{1,0:T(8,128)S(1)} %bitcast.4, f32[8,1024]{1,0:T(8,128)S(1)} %get-tuple-element.18.hub_raw, f32[8,1024]{1,0:T(8,128)S(1)} %get-tuple-element.19.authority_raw), custom_call_target="tpu_custom_call" | custom-call | tf_op jit(solution)/shard_map/finish/pallas_call | solution.py:328
Async XLA Ops:
  0.6 31.9 %copy-start.1 = (s32[256]{0:T(256)S(1)}, s32[256]{0:T(256)}, u32[]{:S(2)}) copy-start(s32[256]{0:T(256)} %slot_s.3) | copy-start | bytes 3076
  0.6 31.9 %copy-start = (s32[256]{0:T(256)S(1)}, s32[256]{0:T(256)}, u32[]{:S(2)}) copy-start(s32[256]{0:T(256)} %row_s.3) | copy-start | bytes 3076

commit v3 on v2

--- a/solution.py
+++ b/solution.py
@@ -1,3 +1,4 @@
+import functools
 import math
 
 import jax
@@ -12,17 +13,18 @@
 GROUP = 8
 COPY_TILES = 32
 STEP_TILES = 64
-VMEM_LIMIT = 24 * 1024 * 1024
+VMEM_LIMIT = 28 * 1024 * 1024
 
 F32 = jnp.float32
 BF16 = jnp.bfloat16
 
 
-def tile_sweep(transposed, count, row_s, slot_s, tiles, source, accum, chunk, group, arrive):
+def tile_sweep(
+    rounds, chunk, group, count, pick, put, tiles, source, accum, before=None, beside=None
+):
     zero_at = source.shape[0] - 1
     columns, edge = source.shape[1:]
     half = group // 2
-    pick, put = (row_s, slot_s) if transposed else (slot_s, row_s)
 
     def one_group(base):
         blocks = []
@@ -40,26 +42,26 @@
             1,
         ).astype(BF16)
         weights = [tiles[base + t] for t in range(group)]
-        outer, inner = (1, 0) if transposed else (0, 1)
         right = jnp.concatenate(
-            [jnp.concatenate(weights[0::2], outer), jnp.concatenate(weights[1::2], outer)], inner
+            [jnp.concatenate(weights[0::2], 1), jnp.concatenate(weights[1::2], 1)], 0
         )
-        product = lax.dot_general(
-            left, right, (((1,), (inner,)), ((), ())), preferred_element_type=F32
-        )
+        product = jnp.dot(left, right, preferred_element_type=F32)
         for t in range(group):
             first = (t % 2) * columns * half + (t // 2) * columns
             lane = (t // 2) * edge
             accum[targets[t]] += product[first : first + columns, lane : lane + edge]
 
     def one_chunk(c, carry):
-        arrive(c)
-
+        if before is not None:
+            before(c)
         for g in range(chunk // group):
             one_group(c * chunk + g * group)
+            if beside is not None:
+                for t in range(group):
+                    beside(c * chunk + g * group + t)
         return carry
 
-    lax.fori_loop(0, (count + chunk - 1) // chunk, one_chunk, 0)
+    lax.fori_loop(0, rounds, one_chunk, 0)
 
 
 def pack_blocks(accum, send, devices, slots_each):
@@ -79,12 +81,13 @@
         slot_total = fetch_list.shape[1]
         slots_each = slot_total // devices
         node_total = hub_start.shape[1] * devices
-        chunk = math.gcd(COPY_TILES, tile_total)
         step = math.gcd(STEP_TILES, tile_total)
+        chunk = math.gcd(COPY_TILES, step)
         group = math.gcd(GROUP, chunk)
         always = min(2, tile_total // chunk)
         rows_each = slots_each * columns
-        assert blocks**slots_each <= 256 and group % 2 == 0
+        rows_first = rows_each + slots_each + slots_each % 2
+        assert group % 2 == 0
 
         smem = pl.BlockSpec(memory_space=pltpu.SMEM)
         vmem = pl.BlockSpec(memory_space=pltpu.VMEM)
@@ -93,7 +96,7 @@
 
         def start_kernel(
             cnt, row_hbm, slot_hbm, fetch_hbm, hub_hbm, tiles,
-            send, kept, row_s, slot_s, fetch, hub, source, accum, sems, small
+            send, kept, flipped, live_count, row_s, slot_s, fetch, hub, source, accum, sems, small
         ):
             def copy(c):
                 span = pl.ds(c * chunk, chunk)
@@ -116,41 +119,47 @@
             accum[...] = jnp.zeros_like(accum)
             source[blocks] = jnp.zeros((columns, edge), F32)
             count = cnt[0]
-            live = (count + chunk - 1) // chunk
+            live_count[...] = jnp.full(live_count.shape, count, jnp.int32)
+            live = (count + step - 1) // step * (step // chunk)
             lax.fori_loop(always, live, begin, 0)
             for part in parts:
                 part.wait()
+
+            def flip(i):
+                flipped[i] = kept[i].T
+
             for b in range(blocks):
                 source[b] = hub[:, b * edge : (b + 1) * edge].astype(BF16).astype(F32)
             tile_sweep(
-                True, count, row_s, slot_s, kept, source, accum, chunk, group,
-                lambda c: copy(c).wait(),
+                live, chunk, group, count, row_s, slot_s, kept, source, accum,
+                lambda c: copy(c).wait(), flip,
             )
             lax.fori_loop(live, always, end, 0)
-            pack_blocks(accum, send, devices, slots_each)
             for p in range(devices):
-                code = fetch[0, p * slots_each]
-                for k in range(1, slots_each):
-                    code = code + fetch[0, p * slots_each + k] * blocks**k
-                send[p, rows_each:, :] = (
-                    jnp.full((columns, edge), code, jnp.int32).astype(F32).astype(BF16)
+                base = p * rows_first
+                both = [accum[p * slots_each + k] for k in range(slots_each)]
+                send[base : base + rows_each] = jnp.concatenate(both, 0).astype(BF16)
+                wanted = [
+                    jnp.full((1, edge), fetch[0, p * slots_each + k % slots_each], jnp.int32)
+                    for k in range(rows_first - rows_each)
+                ]
+                send[base + rows_each : base + rows_first] = (
+                    jnp.concatenate(wanted, 0).astype(F32).astype(BF16)
                 )
 
-        def owner_kernel(got, codes, reply, raw=None, squares=None):
+        def owner_kernel(got_rows, got, first, reply, raw=None, squares=None):
             totals = [jnp.zeros((columns, edge), F32) for _ in range(blocks)]
 
-            def entries(p):
-                code = codes[p, rows_each:, :].astype(F32)
-                wanted = []
-                for k in range(slots_each - 1, 0, -1):
-                    high = jnp.floor(code * (1.0 / blocks**k))
-                    wanted.append(high)
-                    code = code - high * blocks**k
-                return (wanted + [code])[::-1]
+            def wanted_blocks(p):
+                base = p * rows_first
+                rows = first[base + rows_each : base + rows_first].astype(F32)
+                return [
+                    jnp.broadcast_to(rows[k : k + 1], (columns, edge)) for k in range(slots_each)
+                ]
 
             for p in range(devices):
-                wanted = entries(p)
-                values = got[p, :rows_each, :].astype(F32)
+                wanted = wanted_blocks(p)
+                values = got[p * got_rows : p * got_rows + rows_each].astype(F32)
                 for k in range(slots_each):
                     value = values[k * columns : (k + 1) * columns]
                     for b in range(blocks):
@@ -162,7 +171,7 @@
                     square = square + totals[b] * totals[b]
                 squares[...] = square
             for p in range(devices):
-                wanted = entries(p)
+                wanted = wanted_blocks(p)
                 out = []
                 for k in range(slots_each):
                     chosen = totals[0]
@@ -178,14 +187,16 @@
                     source[p * slots_each + k] = both[k * columns : (k + 1) * columns]
             source[slot_total] = jnp.zeros((columns, edge), F32)
 
-        def middle_kernel(cnt, row_s, slot_s, fetched, tiles, send, squares, source, hub, accum, low):
-            count = cnt[0]
+        def middle_kernel(
+            cnt, row_s, slot_s, fetched, tiles, flipped,
+            send, squares, source, hub, accum, low
+        ):
+            count = cnt[0, 0]
+            rounds = (count + step - 1) // step
             load_fetched(fetched, source)
             hub[...] = jnp.zeros_like(hub)
             accum[...] = jnp.zeros_like(accum)
-            tile_sweep(
-                False, count, row_s, slot_s, tiles, source, hub, step, group, lambda c: None
-            )
+            tile_sweep(rounds, step, group, count, slot_s, row_s, flipped, source, hub)
             square = jnp.zeros((columns, edge), F32)
             for b in range(blocks):
                 value = hub[b]
@@ -193,18 +204,18 @@
                 low[b] = value.astype(BF16).astype(F32)
             low[blocks] = jnp.zeros((columns, edge), F32)
             squares[...] = square
-            tile_sweep(
-                True, count, row_s, slot_s, tiles, low, accum, step, group, lambda c: None
-            )
+            tile_sweep(rounds, step, group, count, row_s, slot_s, tiles, low, accum)
             pack_blocks(accum, send, devices, slots_each)
 
-        def last_kernel(cnt, row_s, slot_s, fetched, tiles, first_squares, authority_squares, raw, send, source, hub):
-            count = cnt[0]
+        def last_kernel(
+            cnt, row_s, slot_s, fetched, flipped, first_squares, authority_squares,
+            raw, send, source, hub
+        ):
+            count = cnt[0, 0]
+            rounds = (count + step - 1) // step
             load_fetched(fetched, source)
             hub[...] = jnp.zeros_like(hub)
-            tile_sweep(
-                False, count, row_s, slot_s, tiles, source, hub, step, group, lambda c: None
-            )
+            tile_sweep(rounds, step, group, count, slot_s, row_s, flipped, source, hub)
             largest = jnp.zeros((columns, edge), F32)
             for b in range(blocks):
                 largest = jnp.maximum(largest, jnp.abs(hub[b]))
@@ -273,15 +284,17 @@
 
         small = [tile_count, tile_row, tile_slot]
         operands = small + [fetch_list, hub_start, edge_tiles]
-        send, tiles = pl.pallas_call(
+        send, tiles, flipped, live_count = pl.pallas_call(
             start_kernel,
             name="start",
             out_shape=(
-                shape((devices, rows_each + columns, edge), BF16),
+                shape((devices * rows_first, edge), BF16),
                 shape(edge_tiles.shape, edge_tiles.dtype),
+                shape(edge_tiles.shape, edge_tiles.dtype),
+                shape((1, edge), jnp.int32),
             ),
             in_specs=[smem] + [hbm] * 5,
-            out_specs=(vmem, vmem),
+            out_specs=(vmem,) * 4,
             scratch_shapes=[
                 *[pltpu.SMEM(a.shape, a.dtype) for a in small[1:]],
                 pltpu.SMEM(fetch_list.shape, fetch_list.dtype),
@@ -293,11 +306,13 @@
             ],
             compiler_params=params,
         )(tile_count, *[pltpu.with_memory_space_constraint(a, pltpu.HBM) for a in operands[1:]])
-        first = exchange(send)
+        halves = (devices, rows_first // 2, 2, edge)
+        first = exchange(send.reshape(halves)).reshape(send.shape)
+        small = [live_count, tile_row, tile_slot]
 
         def owner(got, outputs):
             return pl.pallas_call(
-                owner_kernel,
+                functools.partial(owner_kernel, got.shape[0] // devices),
                 name="owner",
                 out_shape=(plain, whole, square_shape)[:outputs],
                 in_specs=[vmem, vmem],
@@ -310,12 +325,12 @@
             middle_kernel,
             name="middle",
             out_shape=(plain, square_shape),
-            in_specs=[smem, smem, smem, vmem, vmem],
+            in_specs=[smem, smem, smem, vmem, vmem, vmem],
             out_specs=(vmem, vmem),
             scratch_shapes=[source_slots, sum_blocks, sum_slots, source_blocks],
             compiler_params=params,
-        )(*small, exchange(reply), tiles)
-        reply, authority_raw, authority_squares = owner(exchange(send), 3)
+        )(*small, exchange(reply), tiles, flipped)
+        reply, authority_raw, authority_squares = owner(exchange(send).reshape(devices * rows_each, edge), 3)
         hub_raw, send = pl.pallas_call(
             last_kernel,
             name="last",
@@ -324,7 +339,7 @@
             out_specs=(vmem, vmem),
             scratch_shapes=[source_slots, sum_blocks],
             compiler_params=params,
-        )(*small, exchange(reply), tiles, first_squares, authority_squares)
+        )(*small, exchange(reply), flipped, first_squares, authority_squares)
         return pl.pallas_call(
             finish_kernel,
             name="finish",

time: 72.6 us -> 69.7 us (0.960)
  blocking collectives: 64.2 us -> 61.3 us
    all_to_all x5, blocking collectives: 64.2 us -> 61.3 us  [exchange(): lax.all_to_all(value, 'rows', split_axis=0, concat_axis=0, tiled=True)]
where the time goes in v3:
time: 69.7 us; the launch traced here: 69.5 us
  blocking collectives  61.3 us (88%)
  Pallas kernels  6.86 us (10%)
  between operations  1.34 us (2%)
    all_to_all x5, blocking collectives, exchange(): lax.all_to_all(value, 'rows', split_axis=0, concat_axis=0, tiled=True)  61.3 us
    pallas_call x1, Pallas kernels, per_device(): pl.pallas_call(start_kernel, name='start', out_shape=(shape((devices * ro...  2.1 us
    pallas_call x1, Pallas kernels, per_device(): pl.pallas_call(middle_kernel, name='middle', out_shape=(plain, square_sha...  1.64 us

profile of v3, /device:TPU:0, one launch (start us, length us, event | category | flops | bytes accessed | tf_op | source)
XLA Modules:
  0.0 69.5 jit_solution(11973149050050670089)
XLA Ops:
  0.6 0.0 copy-start.1
  0.6 0.0 copy-start
  1.3 2.1 %start.1 = (bf16[576,128]{1,0:T(8,128)(2,1)S(1)}, bf16[256,128,128]{2,1,0:T(8,128)(2,1)S(1)}, bf16[256,128,128]{2,1,0:T(8,128)(2,1)S(1)}, s32[1,128]{1,0:T(1,128)S(1)}) custom-call(s32[1]{0:T(128)S(6)} %copy.9.cnt, s32[256]{0:T(256)} %row_s.3, s32[256]{0:T(256)} %slot_s.3, s32[1,64]{1,0:T(1,128)} %fetch_hbm.1, f32[8,1024]{1,0:T(8,128)} %hub_hbm.1, ...), custom_call_target="tpu_custom_call" | custom-call | tf_op jit(solution)/shard_map/start/pallas_call | solution.py:287
  3.4 17.6 %all_to_all.31 = bf16[32,9,2,128]{3,2,1,0:T(2,128)(2,1)S(1)} all-to-all(bf16[32,9,2,128]{3,2,1,0:T(2,128)(2,1)S(1)} %bitcast.11), channel_id=1, replica_groups=mesh['rows'=32] {'rows'}, dimensions={0} | all-to-all | bytes 294912 | tf_op jit(solution)/shard_map/all_to_all | solution.py:283
  21.0 0.6 owner.2
  21.6 10.1 %all_to_all.32.fetched = bf16[32,16,128]{2,1,0:T(8,128)(2,1)S(1)} all-to-all(bf16[32,16,128]{2,1,0:T(8,128)(2,1)S(1)} %owner.2), channel_id=1, replica_groups=mesh['rows'=32] {'rows'}, dimensions={0} | all-to-all | bytes 262144 | tf_op jit(solution)/shard_map/all_to_all | solution.py:283
  31.7 0.0 copy-done.1
  31.7 0.0 copy-done
  31.7 1.6 %middle.1 = (bf16[32,16,128]{2,1,0:T(8,128)(2,1)S(1)}, f32[8,128]{1,0:T(8,128)S(1)}) custom-call(s32[1,128]{1,0:T(1,128)S(1)} %get-tuple-element.13.cnt, s32[256]{0:T(256)S(1)} %copy-done, s32[256]{0:T(256)S(1)} %copy-done.1, bf16[32,16,128]{2,1,0:T(8,128)(2,1)S(1)} %all_to_all.32.fetched, bf16[256,128,128]{2,1,0:T(8,128)(2,1)S(1)} %get-tuple-element.15.tiles, ...), custom_call_target="tpu_custom_call" | custom-call | tf_op jit(solution)/shard_map/middle/pallas_call | solution.py:324
  33.4 13.1 %all_to_all.33 = bf16[32,16,128]{2,1,0:T(8,128)(2,1)S(1)} all-to-all(bf16[32,16,128]{2,1,0:T(8,128)(2,1)S(1)} %get-tuple-element.17), channel_id=1, replica_groups=mesh['rows'=32] {'rows'}, dimensions={0} | all-to-all | bytes 262144 | tf_op jit(solution)/shard_map/all_to_all | solution.py:283
  46.4 0.4 owner.3
  46.8 10.0 %all_to_all.34.fetched = bf16[32,16,128]{2,1,0:T(8,128)(2,1)S(1)} all-to-all(bf16[32,16,128]{2,1,0:T(8,128)(2,1)S(1)} %get-tuple-element.18), channel_id=1, replica_groups=mesh['rows'=32] {'rows'}, dimensions={0} | all-to-all | bytes 262144 | tf_op jit(solution)/shard_map/all_to_all | solution.py:283
  56.8 1.3 %last.1 = (f32[8,1024]{1,0:T(8,128)S(1)}, f32[32,128]{1,0:T(8,128)S(1)}) custom-call(s32[1,128]{1,0:T(1,128)S(1)} %get-tuple-element.13.cnt, s32[256]{0:T(256)S(1)} %copy-done, s32[256]{0:T(256)S(1)} %copy-done.1, bf16[32,16,128]{2,1,0:T(8,128)(2,1)S(1)} %all_to_all.34.fetched, bf16[256,128,128]{2,1,0:T(8,128)(2,1)S(1)} %get-tuple-element.16.flipped, ...), custom_call_target="tpu_custom_call" | custom-call | tf_op jit(solution)/shard_map/last/pallas_call | solution.py:334
  58.1 10.5 %all_to_all.35 = f32[32,1,128]{2,1,0:T(1,128)S(1)} all-to-all(f32[32,1,128]{2,1,0:T(1,128)S(1)} %bitcast.13), channel_id=1, replica_groups=mesh['rows'=32] {'rows'}, dimensions={0} | all-to-all | bytes 32768 | tf_op jit(solution)/shard_map/all_to_all | solution.py:283
  68.6 0.9 %finish.1 = (f32[8,1024]{1,0:T(8,128)}, f32[8,1024]{1,0:T(8,128)}) custom-call(f32[32,128]{1,0:T(8,128)S(1)} %bitcast.12, f32[8,1024]{1,0:T(8,128)S(1)} %get-tuple-element.22.hub_raw, f32[8,1024]{1,0:T(8,128)S(1)} %get-tuple-element.23.authority_raw), custom_call_target="tpu_custom_call" | custom-call | tf_op jit(solution)/shard_map/finish/pallas_call | solution.py:343
Async XLA Ops:
  0.6 31.1 %copy-start.1 = (s32[256]{0:T(256)S(1)}, s32[256]{0:T(256)}, u32[]{:S(2)}) copy-start(s32[256]{0:T(256)} %slot_s.3) | copy-start | bytes 3076
  0.6 31.1 %copy-start = (s32[256]{0:T(256)S(1)}, s32[256]{0:T(256)}, u32[]{:S(2)}) copy-start(s32[256]{0:T(256)} %row_s.3) | copy-start | bytes 3076

commit v4 on v3

--- a/solution.py
+++ b/solution.py
@@ -10,7 +10,7 @@
 
 ITERS = 2
 EPS = 1e-06
-GROUP = 8
+GROUP = 2
 COPY_TILES = 32
 STEP_TILES = 64
 VMEM_LIMIT = 28 * 1024 * 1024
@@ -20,7 +20,7 @@
 
 
 def tile_sweep(
-    rounds, chunk, group, count, pick, put, tiles, source, accum, before=None, beside=None
+    live, chunk, group, count, pick, put, tiles, source, accum, before=None, beside=None
 ):
     zero_at = source.shape[0] - 1
     columns, edge = source.shape[1:]
@@ -61,7 +61,20 @@
                     beside(c * chunk + g * group + t)
         return carry
 
-    lax.fori_loop(0, rounds, one_chunk, 0)
+    chunks = tiles.shape[0] // chunk
+
+    if before is not None:
+        lax.fori_loop(0, live, one_chunk, 0)
+        return
+
+    @pl.when(live == chunks)
+    def _():
+        for c in range(chunks):
+            one_chunk(c, 0)
+
+    @pl.when(live < chunks)
+    def _():
+        lax.fori_loop(0, live, one_chunk, 0)
 
 
 def pack_blocks(accum, send, devices, slots_each):

time: 69.7 us -> 68 us (0.976)
  blocking collectives: 61.3 us -> 59.7 us
    all_to_all x5, blocking collectives: 61.3 us -> 59.7 us  [exchange(): lax.all_to_all(value, 'rows', split_axis=0, concat_axis=0, tiled=True)]
where the time goes in v4:
time: 68 us; the launch traced here: 67.7 us
  blocking collectives  59.7 us (88%)
  Pallas kernels  6.69 us (10%)
  between operations  1.34 us (2%)
    all_to_all x5, blocking collectives, exchange(): lax.all_to_all(value, 'rows', split_axis=0, concat_axis=0, tiled=True)  59.7 us
    pallas_call x1, Pallas kernels, per_device(): pl.pallas_call(start_kernel, name='start', out_shape=(shape((devices * ro...  2.09 us
    pallas_call x1, Pallas kernels, per_device(): pl.pallas_call(middle_kernel, name='middle', out_shape=(plain, square_sha...  1.54 us

profile of v4, /device:TPU:0, one launch (start us, length us, event | category | flops | bytes accessed | tf_op | source)
XLA Modules:
  0.0 67.7 jit_solution(8793385486706854635)
XLA Ops:
  0.6 0.0 copy-start.1
  0.6 0.0 copy-start
  1.3 2.1 %start.1 = (bf16[576,128]{1,0:T(8,128)(2,1)S(1)}, bf16[256,128,128]{2,1,0:T(8,128)(2,1)S(1)}, bf16[256,128,128]{2,1,0:T(8,128)(2,1)S(1)}, s32[1,128]{1,0:T(1,128)S(1)}) custom-call(s32[1]{0:T(128)S(6)} %copy.9.cnt, s32[256]{0:T(256)} %row_s.3, s32[256]{0:T(256)} %slot_s.3, s32[1,64]{1,0:T(1,128)} %fetch_hbm.1, f32[8,1024]{1,0:T(8,128)} %hub_hbm.1, ...), custom_call_target="tpu_custom_call" | custom-call | tf_op jit(solution)/shard_map/start/pallas_call | solution.py:300
  3.4 17.6 %all_to_all.31 = bf16[32,9,2,128]{3,2,1,0:T(2,128)(2,1)S(1)} all-to-all(bf16[32,9,2,128]{3,2,1,0:T(2,128)(2,1)S(1)} %bitcast.11), channel_id=1, replica_groups=mesh['rows'=32] {'rows'}, dimensions={0} | all-to-all | bytes 294912 | tf_op jit(solution)/shard_map/all_to_all | solution.py:296
  21.0 0.6 owner.2
  21.6 10.1 %all_to_all.32.fetched = bf16[32,16,128]{2,1,0:T(8,128)(2,1)S(1)} all-to-all(bf16[32,16,128]{2,1,0:T(8,128)(2,1)S(1)} %owner.2), channel_id=1, replica_groups=mesh['rows'=32] {'rows'}, dimensions={0} | all-to-all | bytes 262144 | tf_op jit(solution)/shard_map/all_to_all | solution.py:296
  31.7 0.0 copy-done.1
  31.7 0.0 copy-done
  31.7 1.5 %middle.1 = (bf16[32,16,128]{2,1,0:T(8,128)(2,1)S(1)}, f32[8,128]{1,0:T(8,128)S(1)}) custom-call(s32[1,128]{1,0:T(1,128)S(1)} %get-tuple-element.13.cnt, s32[256]{0:T(256)S(1)} %copy-done, s32[256]{0:T(256)S(1)} %copy-done.1, bf16[32,16,128]{2,1,0:T(8,128)(2,1)S(1)} %all_to_all.32.fetched, bf16[256,128,128]{2,1,0:T(8,128)(2,1)S(1)} %get-tuple-element.15.tiles, ...), custom_call_target="tpu_custom_call" | custom-call | tf_op jit(solution)/shard_map/middle/pallas_call | solution.py:337
  33.2 12.1 %all_to_all.33 = bf16[32,16,128]{2,1,0:T(8,128)(2,1)S(1)} all-to-all(bf16[32,16,128]{2,1,0:T(8,128)(2,1)S(1)} %get-tuple-element.17), channel_id=1, replica_groups=mesh['rows'=32] {'rows'}, dimensions={0} | all-to-all | bytes 262144 | tf_op jit(solution)/shard_map/all_to_all | solution.py:296
  45.3 0.4 owner.3
  45.6 10.0 %all_to_all.34.fetched = bf16[32,16,128]{2,1,0:T(8,128)(2,1)S(1)} all-to-all(bf16[32,16,128]{2,1,0:T(8,128)(2,1)S(1)} %get-tuple-element.18), channel_id=1, replica_groups=mesh['rows'=32] {'rows'}, dimensions={0} | all-to-all | bytes 262144 | tf_op jit(solution)/shard_map/all_to_all | solution.py:296
  55.6 1.2 %last.1 = (f32[8,1024]{1,0:T(8,128)S(1)}, f32[32,128]{1,0:T(8,128)S(1)}) custom-call(s32[1,128]{1,0:T(1,128)S(1)} %get-tuple-element.13.cnt, s32[256]{0:T(256)S(1)} %copy-done, s32[256]{0:T(256)S(1)} %copy-done.1, bf16[32,16,128]{2,1,0:T(8,128)(2,1)S(1)} %all_to_all.34.fetched, bf16[256,128,128]{2,1,0:T(8,128)(2,1)S(1)} %get-tuple-element.16.flipped, ...), custom_call_target="tpu_custom_call" | custom-call | tf_op jit(solution)/shard_map/last/pallas_call | solution.py:347
  56.8 10.0 %all_to_all.35 = f32[32,1,128]{2,1,0:T(1,128)S(1)} all-to-all(f32[32,1,128]{2,1,0:T(1,128)S(1)} %bitcast.13), channel_id=1, replica_groups=mesh['rows'=32] {'rows'}, dimensions={0} | all-to-all | bytes 32768 | tf_op jit(solution)/shard_map/all_to_all | solution.py:296
  66.8 0.9 %finish.1 = (f32[8,1024]{1,0:T(8,128)}, f32[8,1024]{1,0:T(8,128)}) custom-call(f32[32,128]{1,0:T(8,128)S(1)} %bitcast.12, f32[8,1024]{1,0:T(8,128)S(1)} %get-tuple-element.22.hub_raw, f32[8,1024]{1,0:T(8,128)S(1)} %get-tuple-element.23.authority_raw), custom_call_target="tpu_custom_call" | custom-call | tf_op jit(solution)/shard_map/finish/pallas_call | solution.py:356
Async XLA Ops:
  0.6 31.0 %copy-start.1 = (s32[256]{0:T(256)S(1)}, s32[256]{0:T(256)}, u32[]{:S(2)}) copy-start(s32[256]{0:T(256)} %slot_s.3) | copy-start | bytes 3076
  0.6 31.0 %copy-start = (s32[256]{0:T(256)S(1)}, s32[256]{0:T(256)}, u32[]{:S(2)}) copy-start(s32[256]{0:T(256)} %row_s.3) | copy-start | bytes 3076
